TPU v7x, 8 devices: a whole 2x2x1 slice. The times are simulated.
8 devices in a mesh: dp: 1 (over z), tp: 2 (over y), pp: 4 (over x, core).
Axes of the slice: x: 2, y: 2, z: 1, core: 2. Of those that a mesh axis runs over, the one named last changes fastest.
Arguments:
- x_micro: bfloat16 [8, 12, 512, 768], P(None, 'dp')
- ln1_gain: bfloat16 [4, 768], P('pp')
- ln1_bias: bfloat16 [4, 768], P('pp')
- w_qkv: bfloat16 [4, 3, 768, 12, 64], P('pp', None, None, 'tp')
- b_qkv: bfloat16 [4, 3, 12, 64], P('pp', None, 'tp')
- w_out: bfloat16 [4, 12, 64, 768], P('pp', 'tp')
- b_out: bfloat16 [4, 768], P('pp')
- ln2_gain: bfloat16 [4, 768], P('pp')
- ln2_bias: bfloat16 [4, 768], P('pp')
- w_up: bfloat16 [4, 768, 3072], P('pp', None, 'tp')
- b_up: bfloat16 [4, 3072], P('pp', 'tp')
- w_down: bfloat16 [4, 3072, 768], P('pp', 'tp')
- b_down: bfloat16 [4, 768], P('pp')
Outputs:
- output: bfloat16 [4, 8, 12, 512, 768], P('pp', None, 'dp')
All inputs are finite; a program needn't handle non-finite values.
Results may differ from a plain program's by a relative error of at most 0.0177418.
Values are sent between devices in bfloat16 or wider.
A program may use at most 1 GiB of HBM per device.

v0:
```python
import jax
import jax.numpy as jnp
from jax import lax
from jax.sharding import PartitionSpec as P

LN_EPS = 1e-5


def layer_norm(act_in, gain_vec, bias_vec):
    act_f32 = act_in.astype(jnp.float32)
    row_mean = jnp.mean(act_f32, axis=-1, keepdims=True)
    centered = act_f32 - row_mean
    row_var = jnp.mean(centered * centered, axis=-1, keepdims=True)
    normed = centered * lax.rsqrt(row_var + LN_EPS)
    return (normed * gain_vec.astype(jnp.float32) + bias_vec.astype(jnp.float32)).astype(jnp.bfloat16)


def stage_layer(act_in, layer_params):
    ln1_gain, ln1_bias, w_qkv, b_qkv, w_out, b_out, ln2_gain, ln2_bias, w_up, b_up, w_down, b_down = layer_params
    head_dim = w_qkv.shape[-1]
    seq_len = act_in.shape[1]
    normed_in = layer_norm(act_in, ln1_gain, ln1_bias)
    qkv_proj = (jnp.einsum('bsd,cdhe->cbshe', normed_in, w_qkv, preferred_element_type=jnp.float32) + b_qkv[:, None, None].astype(jnp.float32)).astype(jnp.bfloat16)
    scores = jnp.einsum('bqhe,bkhe->bhqk', qkv_proj[0], qkv_proj[1], preferred_element_type=jnp.float32) * (head_dim ** -0.5)
    causal = lax.broadcasted_iota(jnp.int32, (seq_len, seq_len), 0) >= lax.broadcasted_iota(jnp.int32, (seq_len, seq_len), 1)
    attn_probs = jax.nn.softmax(jnp.where(causal, scores, -1e30), axis=-1).astype(jnp.bfloat16)
    context = jnp.einsum('bhqk,bkhe->bqhe', attn_probs, qkv_proj[2], preferred_element_type=jnp.float32).astype(jnp.bfloat16)
    attn_part = jnp.einsum('crif,ife->cre', context, w_out, preferred_element_type=jnp.float32).astype(jnp.bfloat16)
    attn_out = (lax.psum(attn_part, 'tp').astype(jnp.float32) + b_out.astype(jnp.float32)).astype(jnp.bfloat16)
    resid_mid = (act_in.astype(jnp.float32) + attn_out.astype(jnp.float32)).astype(jnp.bfloat16)
    normed_mid = layer_norm(resid_mid, ln2_gain, ln2_bias)
    hidden_up = jax.nn.gelu(jnp.einsum('bsd,df->bsf', normed_mid, w_up, preferred_element_type=jnp.float32) + b_up.astype(jnp.float32), approximate=True).astype(jnp.bfloat16)
    mlp_part = jnp.einsum('bsf,fd->bsd', hidden_up, w_down, preferred_element_type=jnp.float32).astype(jnp.bfloat16)
    mlp_out = (lax.psum(mlp_part, 'tp').astype(jnp.float32) + b_down.astype(jnp.float32)).astype(jnp.bfloat16)
    return (resid_mid.astype(jnp.float32) + mlp_out.astype(jnp.float32)).astype(jnp.bfloat16)


def solution(mesh):
    stages = mesh.shape['pp']
    shift_pairs = [(source_idx, source_idx + 1) for source_idx in range(stages - 1)]
    weight_specs = (
        P('pp', None), P('pp', None),
        P('pp', None, None, 'tp', None), P('pp', None, 'tp', None),
        P('pp', 'tp', None, None), P('pp', None),
        P('pp', None), P('pp', None),
        P('pp', None, 'tp'), P('pp', 'tp'),
        P('pp', 'tp', None), P('pp', None),
    )

    def local_run(x_micro, ln1_gain, ln1_bias, w_qkv, b_qkv, w_out, b_out, ln2_gain, ln2_bias, w_up, b_up, w_down, b_down):
        layer_params = tuple(stacked[0] for stacked in (ln1_gain, ln1_bias, w_qkv, b_qkv, w_out, b_out, ln2_gain, ln2_bias, w_up, b_up, w_down, b_down))
        micro_count = x_micro.shape[0]
        stage_idx = lax.axis_index('pp')

        def time_step(tick, loop_state):
            received, out_buf = loop_state
            first_in = lax.dynamic_index_in_dim(x_micro, jnp.minimum(tick, micro_count - 1), 0, keepdims=False)
            stage_in = jnp.where(stage_idx == 0, first_in, received)
            stage_out = stage_layer(stage_in, layer_params)
            micro_idx = tick - stage_idx
            is_valid = (micro_idx >= 0) & (micro_idx < micro_count)
            slot_idx = jnp.clip(micro_idx, 0, micro_count - 1)
            old_slot = lax.dynamic_index_in_dim(out_buf, slot_idx, 0, keepdims=False)
            out_buf = lax.dynamic_update_index_in_dim(out_buf, jnp.where(is_valid, stage_out, old_slot), slot_idx, 0)
            received = lax.ppermute(stage_out, 'pp', shift_pairs)
            return received, out_buf

        start_state = (jnp.zeros(x_micro.shape[1:], jnp.bfloat16), jnp.zeros(x_micro.shape, jnp.bfloat16))
        final_recv, out_buf = lax.fori_loop(0, micro_count + stages - 1, time_step, start_state)
        return out_buf[None]

    return jax.shard_map(local_run, mesh=mesh, in_specs=(P(None, 'dp', None, None),) + weight_specs, out_specs=P('pp', None, 'dp', None, None), check_vma=False)
```

profile of v0, /device:TPU:3, one launch (start us, length us, event | category | flops | bytes accessed | tf_op | source)
XLA Modules:
  0.0 7742.2 jit_solution(7386377908709991963)
XLA Ops:
  42.5 7692.9 %while.16 = (s32[]{:T(128)}, bf16[12,512,768]{2,1,0:T(8,128)(2,1)}, bf16[8,12,512,768]{3,2,1,0:T(8,128)(2,1)}, pred[]{:T(512)}, bf16[8,12,512,768]{3,2,1,0:T(8,1...) while((s32[]{:T(128)}, bf16[12,512,768]{2,1,0:T(8,128)(2,1)}, ...), condition=%wide.region_9.10_spmd, body=%wide.region_0.9_spmd.sunk | while | flops 48750411776 | bytes 657290176 | solution.py:69
  139.5 215.5 %all-reduce.3.cloned.1.call-done = bf16[12,512,768]{2,1,0:T(8,128)(2,1)} async-done(((bf16[12,512,768]{2,1,0:T(8,128)(2,1)}), bf16[12,512,768]{2,1,0:T(8,128)(2,1)}) %all-reduce.3.cloned.1.call-update) | async-done | bytes 9437200 | tf_op jit(solution)/shard_map/while/body/eval_jaxpr/psum | solution.py:29
  419.6 206.9 %all-reduce.5.cloned.1.call-done = bf16[12,512,768]{2,1,0:T(8,128)(2,1)} async-done(((bf16[12,512,768]{2,1,0:T(8,128)(2,1)}), bf16[12,512,768]{2,1,0:T(8,128)(2,1)}) %all-reduce.5.cloned.1.call-update) | async-done | bytes 9437200 | tf_op jit(solution)/shard_map/while/body/eval_jaxpr/psum | solution.py:34
  693.8 33.9 fusion.110
  758.5 303.9 %all-reduce.3.cloned.1.call-done = bf16[12,512,768]{2,1,0:T(8,128)(2,1)} async-done(((bf16[12,512,768]{2,1,0:T(8,128)(2,1)}), bf16[12,512,768]{2,1,0:T(8,128)(2,1)}) %all-reduce.3.cloned.1.call-update) | async-done | bytes 9437200 | tf_op jit(solution)/shard_map/while/body/eval_jaxpr/psum | solution.py:29
  1127.0 206.9 %all-reduce.5.cloned.1.call-done = bf16[12,512,768]{2,1,0:T(8,128)(2,1)} async-done(((bf16[12,512,768]{2,1,0:T(8,128)(2,1)}), bf16[12,512,768]{2,1,0:T(8,128)(2,1)}) %all-reduce.5.cloned.1.call-update) | async-done | bytes 9437200 | tf_op jit(solution)/shard_map/while/body/eval_jaxpr/psum | solution.py:34
  1465.9 303.9 %all-reduce.3.cloned.1.call-done = bf16[12,512,768]{2,1,0:T(8,128)(2,1)} async-done(((bf16[12,512,768]{2,1,0:T(8,128)(2,1)}), bf16[12,512,768]{2,1,0:T(8,128)(2,1)}) %all-reduce.3.cloned.1.call-update) | async-done | bytes 9437200 | tf_op jit(solution)/shard_map/while/body/eval_jaxpr/psum | solution.py:29
  1834.4 206.9 %all-reduce.5.cloned.1.call-done = bf16[12,512,768]{2,1,0:T(8,128)(2,1)} async-done(((bf16[12,512,768]{2,1,0:T(8,128)(2,1)}), bf16[12,512,768]{2,1,0:T(8,128)(2,1)}) %all-reduce.5.cloned.1.call-update) | async-done | bytes 9437200 | tf_op jit(solution)/shard_map/while/body/eval_jaxpr/psum | solution.py:34
  2173.3 303.9 %all-reduce.3.cloned.1.call-done = bf16[12,512,768]{2,1,0:T(8,128)(2,1)} async-done(((bf16[12,512,768]{2,1,0:T(8,128)(2,1)}), bf16[12,512,768]{2,1,0:T(8,128)(2,1)}) %all-reduce.3.cloned.1.call-update) | async-done | bytes 9437200 | tf_op jit(solution)/shard_map/while/body/eval_jaxpr/psum | solution.py:29
  2541.8 206.9 %all-reduce.5.cloned.1.call-done = bf16[12,512,768]{2,1,0:T(8,128)(2,1)} async-done(((bf16[12,512,768]{2,1,0:T(8,128)(2,1)}), bf16[12,512,768]{2,1,0:T(8,128)(2,1)}) %all-reduce.5.cloned.1.call-update) | async-done | bytes 9437200 | tf_op jit(solution)/shard_map/while/body/eval_jaxpr/psum | solution.py:34
  2880.7 303.9 %all-reduce.3.cloned.1.call-done = bf16[12,512,768]{2,1,0:T(8,128)(2,1)} async-done(((bf16[12,512,768]{2,1,0:T(8,128)(2,1)}), bf16[12,512,768]{2,1,0:T(8,128)(2,1)}) %all-reduce.3.cloned.1.call-update) | async-done | bytes 9437200 | tf_op jit(solution)/shard_map/while/body/eval_jaxpr/psum | solution.py:29
  3249.1 206.9 %all-reduce.5.cloned.1.call-done = bf16[12,512,768]{2,1,0:T(8,128)(2,1)} async-done(((bf16[12,512,768]{2,1,0:T(8,128)(2,1)}), bf16[12,512,768]{2,1,0:T(8,128)(2,1)}) %all-reduce.5.cloned.1.call-update) | async-done | bytes 9437200 | tf_op jit(solution)/shard_map/while/body/eval_jaxpr/psum | solution.py:34
  3588.0 303.9 %all-reduce.3.cloned.1.call-done = bf16[12,512,768]{2,1,0:T(8,128)(2,1)} async-done(((bf16[12,512,768]{2,1,0:T(8,128)(2,1)}), bf16[12,512,768]{2,1,0:T(8,128)(2,1)}) %all-reduce.3.cloned.1.call-update) | async-done | bytes 9437200 | tf_op jit(solution)/shard_map/while/body/eval_jaxpr/psum | solution.py:29
  3956.5 206.9 %all-reduce.5.cloned.1.call-done = bf16[12,512,768]{2,1,0:T(8,128)(2,1)} async-done(((bf16[12,512,768]{2,1,0:T(8,128)(2,1)}), bf16[12,512,768]{2,1,0:T(8,128)(2,1)}) %all-reduce.5.cloned.1.call-update) | async-done | bytes 9437200 | tf_op jit(solution)/shard_map/while/body/eval_jaxpr/psum | solution.py:34
  4295.4 303.9 %all-reduce.3.cloned.1.call-done = bf16[12,512,768]{2,1,0:T(8,128)(2,1)} async-done(((bf16[12,512,768]{2,1,0:T(8,128)(2,1)}), bf16[12,512,768]{2,1,0:T(8,128)(2,1)}) %all-reduce.3.cloned.1.call-update) | async-done | bytes 9437200 | tf_op jit(solution)/shard_map/while/body/eval_jaxpr/psum | solution.py:29
  4663.9 206.9 %all-reduce.5.cloned.1.call-done = bf16[12,512,768]{2,1,0:T(8,128)(2,1)} async-done(((bf16[12,512,768]{2,1,0:T(8,128)(2,1)}), bf16[12,512,768]{2,1,0:T(8,128)(2,1)}) %all-reduce.5.cloned.1.call-update) | async-done | bytes 9437200 | tf_op jit(solution)/shard_map/while/body/eval_jaxpr/psum | solution.py:34
  5002.8 303.9 %all-reduce.3.cloned.1.call-done = bf16[12,512,768]{2,1,0:T(8,128)(2,1)} async-done(((bf16[12,512,768]{2,1,0:T(8,128)(2,1)}), bf16[12,512,768]{2,1,0:T(8,128)(2,1)}) %all-reduce.3.cloned.1.call-update) | async-done | bytes 9437200 | tf_op jit(solution)/shard_map/while/body/eval_jaxpr/psum | solution.py:29
  5371.3 206.9 %all-reduce.5.cloned.1.call-done = bf16[12,512,768]{2,1,0:T(8,128)(2,1)} async-done(((bf16[12,512,768]{2,1,0:T(8,128)(2,1)}), bf16[12,512,768]{2,1,0:T(8,128)(2,1)}) %all-reduce.5.cloned.1.call-update) | async-done | bytes 9437200 | tf_op jit(solution)/shard_map/while/body/eval_jaxpr/psum | solution.py:34
  5710.2 303.9 %all-reduce.3.cloned.1.call-done = bf16[12,512,768]{2,1,0:T(8,128)(2,1)} async-done(((bf16[12,512,768]{2,1,0:T(8,128)(2,1)}), bf16[12,512,768]{2,1,0:T(8,128)(2,1)}) %all-reduce.3.cloned.1.call-update) | async-done | bytes 9437200 | tf_op jit(solution)/shard_map/while/body/eval_jaxpr/psum | solution.py:29
  6078.7 206.9 %all-reduce.5.cloned.1.call-done = bf16[12,512,768]{2,1,0:T(8,128)(2,1)} async-done(((bf16[12,512,768]{2,1,0:T(8,128)(2,1)}), bf16[12,512,768]{2,1,0:T(8,128)(2,1)}) %all-reduce.5.cloned.1.call-update) | async-done | bytes 9437200 | tf_op jit(solution)/shard_map/while/body/eval_jaxpr/psum | solution.py:34
  6417.6 303.9 %all-reduce.3.cloned.1.call-done = bf16[12,512,768]{2,1,0:T(8,128)(2,1)} async-done(((bf16[12,512,768]{2,1,0:T(8,128)(2,1)}), bf16[12,512,768]{2,1,0:T(8,128)(2,1)}) %all-reduce.3.cloned.1.call-update) | async-done | bytes 9437200 | tf_op jit(solution)/shard_map/while/body/eval_jaxpr/psum | solution.py:29
  6786.1 206.9 %all-reduce.5.cloned.1.call-done = bf16[12,512,768]{2,1,0:T(8,128)(2,1)} async-done(((bf16[12,512,768]{2,1,0:T(8,128)(2,1)}), bf16[12,512,768]{2,1,0:T(8,128)(2,1)}) %all-reduce.5.cloned.1.call-update) | async-done | bytes 9437200 | tf_op jit(solution)/shard_map/while/body/eval_jaxpr/psum | solution.py:34
  7125.0 303.9 %all-reduce.3.cloned.1.call-done = bf16[12,512,768]{2,1,0:T(8,128)(2,1)} async-done(((bf16[12,512,768]{2,1,0:T(8,128)(2,1)}), bf16[12,512,768]{2,1,0:T(8,128)(2,1)}) %all-reduce.3.cloned.1.call-update) | async-done | bytes 9437200 | tf_op jit(solution)/shard_map/while/body/eval_jaxpr/psum | solution.py:29
  7493.5 206.9 %all-reduce.5.cloned.1.call-done = bf16[12,512,768]{2,1,0:T(8,128)(2,1)} async-done(((bf16[12,512,768]{2,1,0:T(8,128)(2,1)}), bf16[12,512,768]{2,1,0:T(8,128)(2,1)}) %all-reduce.5.cloned.1.call-update) | async-done | bytes 9437200 | tf_op jit(solution)/shard_map/while/body/eval_jaxpr/psum | solution.py:34
  (674 shorter events, 2160.8 us)
Async XLA Ops:
  42.5 312.4 %all-reduce.3.cloned.1.call-start = ((), (), s32[]{:S(2)}) async-start(), calls=%async_computation | async-start | bytes 18874368 | tf_op jit(solution)/shard_map/while/body/eval_jaxpr/psum | solution.py:29
  139.3 487.2 %all-reduce.5.cloned.1.call-start = ((), (), s32[]{:S(2)}) async-start(), calls=%async_computation.1 | async-start | bytes 18874368 | tf_op jit(solution)/shard_map/while/body/eval_jaxpr/psum | solution.py:34
  661.5 400.8 %all-reduce.3.cloned.1.call-start = ((), (), s32[]{:S(2)}) async-start(), calls=%async_computation | async-start | bytes 18874368 | tf_op jit(solution)/shard_map/while/body/eval_jaxpr/psum | solution.py:29
  758.4 575.6 %all-reduce.5.cloned.1.call-start = ((), (), s32[]{:S(2)}) async-start(), calls=%async_computation.1 | async-start | bytes 18874368 | tf_op jit(solution)/shard_map/while/body/eval_jaxpr/psum | solution.py:34
  1368.9 400.8 %all-reduce.3.cloned.1.call-start = ((), (), s32[]{:S(2)}) async-start(), calls=%async_computation | async-start | bytes 18874368 | tf_op jit(solution)/shard_map/while/body/eval_jaxpr/psum | solution.py:29
  1465.7 575.6 %all-reduce.5.cloned.1.call-start = ((), (), s32[]{:S(2)}) async-start(), calls=%async_computation.1 | async-start | bytes 18874368 | tf_op jit(solution)/shard_map/while/body/eval_jaxpr/psum | solution.py:34
  2076.3 400.8 %all-reduce.3.cloned.1.call-start = ((), (), s32[]{:S(2)}) async-start(), calls=%async_computation | async-start | bytes 18874368 | tf_op jit(solution)/shard_map/while/body/eval_jaxpr/psum | solution.py:29
  2173.1 575.6 %all-reduce.5.cloned.1.call-start = ((), (), s32[]{:S(2)}) async-start(), calls=%async_computation.1 | async-start | bytes 18874368 | tf_op jit(solution)/shard_map/while/body/eval_jaxpr/psum | solution.py:34
  2766.7 16.9 collective-permute-start
  2783.7 400.8 %all-reduce.3.cloned.1.call-start = ((), (), s32[]{:S(2)}) async-start(), calls=%async_computation | async-start | bytes 18874368 | tf_op jit(solution)/shard_map/while/body/eval_jaxpr/psum | solution.py:29
  2880.5 575.6 %all-reduce.5.cloned.1.call-start = ((), (), s32[]{:S(2)}) async-start(), calls=%async_computation.1 | async-start | bytes 18874368 | tf_op jit(solution)/shard_map/while/body/eval_jaxpr/psum | solution.py:34
  3474.1 16.9 collective-permute-start
  3491.1 400.8 %all-reduce.3.cloned.1.call-start = ((), (), s32[]{:S(2)}) async-start(), calls=%async_computation | async-start | bytes 18874368 | tf_op jit(solution)/shard_map/while/body/eval_jaxpr/psum | solution.py:29
  3587.9 575.6 %all-reduce.5.cloned.1.call-start = ((), (), s32[]{:S(2)}) async-start(), calls=%async_computation.1 | async-start | bytes 18874368 | tf_op jit(solution)/shard_map/while/body/eval_jaxpr/psum | solution.py:34
  4198.5 400.8 %all-reduce.3.cloned.1.call-start = ((), (), s32[]{:S(2)}) async-start(), calls=%async_computation | async-start | bytes 18874368 | tf_op jit(solution)/shard_map/while/body/eval_jaxpr/psum | solution.py:29
  4295.3 575.6 %all-reduce.5.cloned.1.call-start = ((), (), s32[]{:S(2)}) async-start(), calls=%async_computation.1 | async-start | bytes 18874368 | tf_op jit(solution)/shard_map/while/body/eval_jaxpr/psum | solution.py:34
  4905.9 400.8 %all-reduce.3.cloned.1.call-start = ((), (), s32[]{:S(2)}) async-start(), calls=%async_computation | async-start | bytes 18874368 | tf_op jit(solution)/shard_map/while/body/eval_jaxpr/psum | solution.py:29
  5002.7 575.6 %all-reduce.5.cloned.1.call-start = ((), (), s32[]{:S(2)}) async-start(), calls=%async_computation.1 | async-start | bytes 18874368 | tf_op jit(solution)/shard_map/while/body/eval_jaxpr/psum | solution.py:34
  5613.2 400.8 %all-reduce.3.cloned.1.call-start = ((), (), s32[]{:S(2)}) async-start(), calls=%async_computation | async-start | bytes 18874368 | tf_op jit(solution)/shard_map/while/body/eval_jaxpr/psum | solution.py:29
  5710.1 575.6 %all-reduce.5.cloned.1.call-start = ((), (), s32[]{:S(2)}) async-start(), calls=%async_computation.1 | async-start | bytes 18874368 | tf_op jit(solution)/shard_map/while/body/eval_jaxpr/psum | solution.py:34
  6320.6 400.8 %all-reduce.3.cloned.1.call-start = ((), (), s32[]{:S(2)}) async-start(), calls=%async_computation | async-start | bytes 18874368 | tf_op jit(solution)/shard_map/while/body/eval_jaxpr/psum | solution.py:29
  6417.4 575.6 %all-reduce.5.cloned.1.call-start = ((), (), s32[]{:S(2)}) async-start(), calls=%async_computation.1 | async-start | bytes 18874368 | tf_op jit(solution)/shard_map/while/body/eval_jaxpr/psum | solution.py:34
  7028.0 400.8 %all-reduce.3.cloned.1.call-start = ((), (), s32[]{:S(2)}) async-start(), calls=%async_computation | async-start | bytes 18874368 | tf_op jit(solution)/shard_map/while/body/eval_jaxpr/psum | solution.py:29
  7124.8 575.6 %all-reduce.5.cloned.1.call-start = ((), (), s32[]{:S(2)}) async-start(), calls=%async_computation.1 | async-start | bytes 18874368 | tf_op jit(solution)/shard_map/while/body/eval_jaxpr/psum | solution.py:34
  (177 other events, 16796.7 us)
Sparse Core Ops, SparseCore 0:
  139.5 215.4 all-reduce.2
  411.7 214.7 all-reduce.4
  758.5 303.8 all-reduce.2
  1119.1 214.7 all-reduce.4
  1465.9 303.8 all-reduce.2
  1826.5 214.7 all-reduce.4
  2173.3 303.8 all-reduce.2
  2533.9 214.7 all-reduce.4
  2880.6 303.8 all-reduce.2
  3241.3 214.7 all-reduce.4
  3588.0 303.8 all-reduce.2
  3948.7 214.7 all-reduce.4
  4295.4 303.8 all-reduce.2
  4656.0 214.7 all-reduce.4
  5002.8 303.8 all-reduce.2
  5363.4 214.7 all-reduce.4
  5710.2 303.8 all-reduce.2
  6070.8 214.7 all-reduce.4
  6417.6 303.8 all-reduce.2
  6778.2 214.7 all-reduce.4
  7124.9 303.8 all-reduce.2
  7485.6 214.7 all-reduce.4
where the time goes:
time: 7830 us; the launch traced here: 7740 us
  waiting for transfers between devices  5700 us (73%)
  matrix products  1390 us (18%)
  other arithmetic  458 us (6%)
  local copies, waits for them, and re-layouts  156 us (2%)
    psum x11, waiting for transfers between devices, stage_layer(): lax.psum(attn_part, 'tp').astype(jnp.float32) + b_out.astype(jnp.float32)  3250 us
    psum x11, waiting for transfers between devices, stage_layer(): lax.psum(mlp_part, 'tp').astype(jnp.float32) + b_down.astype(jnp.float32)  2280 us
    sub x11, matrix products, stage_layer(): jax.nn.softmax(jnp.where(causal, scores, -1e+30), axis=-1)  373 us
    dot_general x11, matrix products, stage_layer(): jnp.einsum('crif,ife->cre', context, w_out, preferred_element_type=jnp.fl...  337 us
    dot_general x11, matrix products, stage_layer(): jnp.einsum('bsd,df->bsf', normed_mid, w_up, preferred_element_type=jnp.fl...  277 us
    dot_general x11, matrix products, stage_layer(): jnp.einsum('bsf,fd->bsd', hidden_up, w_down, preferred_element_type=jnp.f...  217 us
    dynamic_update_slice x11, other arithmetic, time_step(): lax.dynamic_update_index_in_dim(out_buf, jnp.where(is_valid, stage_out, o...  198 us
    dot_general x11, matrix products, stage_layer(): jnp.einsum('bsd,cdhe->cbshe', normed_in, w_qkv, preferred_element_type=jn...  188 us
  transfers between devices with their start and end apart: 33, of which 33 were waited for; matrix products, arithmetic and copies ran while one was open for 1% of the time, Pallas kernels for 0%

commit v1 on v0

v1 whole, which is shorter than its diff:
```python
import functools
import math

import jax
import jax.numpy as jnp
from jax import lax
from jax.experimental import pallas as pl
from jax.experimental.pallas import tpu as pltpu
from jax.sharding import PartitionSpec as P

F32 = jnp.float32
BF16 = jnp.bfloat16
MESH = pl.DeviceIdType.MESH
LN_EPS = 1e-5
N_DUP = 0
IN_SLOTS = 3
OUT_SLOTS = 2
QUERY_BLOCK = 256
COL_BLOCK = 256
GELU_C0 = math.sqrt(2.0 / math.pi)
GELU_C1 = GELU_C0 * 0.044715


def dot(a, b, ca=1, cb=0):
    return lax.dot_general(a, b, (((ca,), (cb,)), ((), ())), preferred_element_type=F32)


def layer_norm(x, gain, bias):
    x = x.astype(F32)
    mean = jnp.mean(x, axis=-1, keepdims=True)
    centered = x - mean
    var = jnp.mean(centered * centered, axis=-1, keepdims=True)
    return (centered * lax.rsqrt(var + LN_EPS) * gain.astype(F32) + bias.astype(F32)).astype(BF16)


def gelu(z):
    half = 0.5 * z
    return half + half * jnp.tanh(z * (GELU_C0 + GELU_C1 * (z * z)))


def attention(qkv, ctx, head_dim):
    seq, width = ctx.shape
    pair = 2 * head_dim
    scale = head_dim**-0.5 * math.log2(math.e)
    first = lax.broadcasted_iota(jnp.int32, (1, pair), 1) < head_dim
    zero = jnp.zeros((), BF16)
    block = QUERY_BLOCK
    rows = lax.broadcasted_iota(jnp.int32, (block, block), 0)
    cols = lax.broadcasted_iota(jnp.int32, (block, block), 1)
    keep = jnp.concatenate([rows >= cols, rows >= cols], axis=0)
    for p in range(width // pair):
        lanes = slice(p * pair, (p + 1) * pair)
        keys = qkv[:, width + p * pair : width + (p + 1) * pair]
        values = qkv[:, 2 * width + p * pair : 2 * width + (p + 1) * pair]
        for q0 in range(0, seq, block):
            q = qkv[q0 : q0 + block, lanes]
            q = jnp.concatenate([jnp.where(first, q, zero), jnp.where(first, zero, q)], axis=0)
            scores = dot(q, keys[: q0 + block], 1, 1)
            diag = jnp.where(keep, scores[:, q0:], -1e30)
            scores = jnp.concatenate([scores[:, :q0], diag], axis=1) if q0 else diag
            top = jnp.max(scores, axis=-1, keepdims=True)
            probs = jnp.exp2((scores - top) * scale)
            total = jnp.sum(probs, axis=-1, keepdims=True)
            out = dot(probs.astype(BF16), values[: q0 + block]) * (1.0 / total)
            ctx[q0 : q0 + block, lanes] = jnp.where(first, out[:block], out[block:]).astype(BF16)


def project_residual(lhs, weight, bias, resid, out):
    for n in range(0, out.shape[1], COL_BLOCK):
        cols = slice(n, n + COL_BLOCK)
        part = (dot(lhs[...], weight[:, cols]) + bias[:, cols].astype(F32)).astype(BF16)
        out[:, cols] = (resid[:, cols].astype(F32) + part.astype(F32)).astype(BF16)


def one_layer(x, y, w, s, head_dim):
    width = x.shape[1]
    s["h"][...] = layer_norm(x[...], w["g1"][...], w["c1"][...])
    for n in range(0, 3 * width, COL_BLOCK):
        cols = slice(n, n + COL_BLOCK)
        s["qkv"][:, cols] = (dot(s["h"][...], w["qkv"][:, cols]) + w["bqkv"][:, cols]).astype(BF16)
    attention(s["qkv"], s["ctx"], head_dim)
    project_residual(s["ctx"], w["out"], w["bout"], x, s["x1"])
    s["h"][...] = layer_norm(s["x1"][...], w["g2"][...], w["c2"][...])
    half = w["up"].shape[2]
    for t in range(2):
        for n in range(0, half, COL_BLOCK):
            z = dot(s["h"][...], w["up"][t, :, n : n + COL_BLOCK]) + w["bup"][t, :, n : n + COL_BLOCK].astype(F32)
            s["u"][:, t * half + n : t * half + n + COL_BLOCK] = gelu(z).astype(BF16)
    project_residual(s["u"], w["down"], w["bdown"], s["x1"], y)


def kernel(
    cfg,
    x_hbm, g1, c1, bout, g2, c2, bdown, qkv_half, bqkv_half, out_half, up_half, bup_half, down_half,
    out_hbm,
    w_qkv, b_qkv_raw, b_qkv, w_out, w_up, b_up, w_down,
    x_in, y_out, h, qkv, ctx, x1, u,
    w_local, w_send, w_recv, in_sem, store_sem, hop_sem, side_send, side_recv, credit,
):
    stages, n_single, n_dup, head_dim = cfg
    total = n_single + n_dup
    t = lax.axis_index("tp")
    p = lax.axis_index("pp")
    width = x_hbm.shape[2]
    half_width = width // 2
    other = {"tp": 1 - t}
    after = {"pp": lax.rem(p + 1, stages)}
    before = {"pp": lax.rem(p + stages - 1, stages)}

    barrier = pltpu.get_barrier_semaphore()
    for peer in (other, after, before):
        pl.semaphore_signal(barrier, inc=1, device_id=peer, device_id_type=MESH)
    pl.semaphore_wait(barrier, 3)

    pieces = []
    for c in range(3):
        at = pl.multiple_of(c * width + t * half_width, 128)
        pieces.append((qkv_half.at[c], w_qkv.at[:, pl.ds(at, half_width)]))
    pieces.append((bqkv_half, b_qkv_raw.at[t]))
    pieces.append((out_half, w_out.at[pl.ds(pl.multiple_of(t * half_width, 128), half_width)]))
    pieces.append((up_half, w_up.at[t]))
    pieces.append((bup_half, b_up.at[t]))
    pieces.append((down_half, w_down.at[pl.ds(pl.multiple_of(t * down_half.shape[0], 128), down_half.shape[0])]))
    copies = []
    for i, (src, dst) in enumerate(pieces):
        far = pltpu.make_async_remote_copy(src, dst, w_send.at[i], w_recv.at[i], device_id=other, device_id_type=MESH)
        near = pltpu.make_async_copy(src, dst, w_local.at[i])
        far.start()
        near.start()
        copies.append((far, near))

    def row_of(n):
        dup = n // n_single
        return n + (1 - dup) * t * n_single + dup * n_single

    def load(n):
        slot = lax.rem(n, IN_SLOTS)
        return pltpu.make_async_copy(x_hbm.at[row_of(n)], x_in.at[slot], in_sem.at[slot])

    def store(n):
        slot = lax.rem(n, OUT_SLOTS)
        return pltpu.make_async_copy(y_out.at[slot], out_hbm.at[row_of(n)], store_sem.at[slot])

    def hop(n):
        src, dst = lax.rem(n, OUT_SLOTS), lax.rem(n, IN_SLOTS)
        return pltpu.make_async_remote_copy(
            y_out.at[src], x_in.at[dst], hop_sem.at[src], in_sem.at[dst], device_id=after, device_id_type=MESH
        )

    def side(n):
        row = row_of(n)
        return pltpu.make_async_remote_copy(
            out_hbm.at[row], out_hbm.at[row], side_send.at[n], side_recv.at[n], device_id=other, device_id_type=MESH
        )

    @pl.when(p == 0)
    def _():
        load(0).start()

    for far, near in copies:
        near.wait()
        far.wait_recv()
    for c in range(3):
        for k in range(2):
            at = c * width + k * half_width
            b_qkv[:, at : at + half_width] = b_qkv_raw[k, :, c * half_width : (c + 1) * half_width].astype(F32)

    weights = dict(
        g1=g1, c1=c1, qkv=w_qkv, bqkv=b_qkv, out=w_out, bout=bout, g2=g2, c2=c2,
        up=w_up, bup=b_up, down=w_down, bdown=bdown,
    )
    scratch = dict(h=h, qkv=qkv, ctx=ctx, x1=x1, u=u)

    def step(n, carry):
        in_slot, out_slot = lax.rem(n, IN_SLOTS), lax.rem(n, OUT_SLOTS)
        load(n).wait()

        @pl.when((p == 0) & (n + 1 < total))
        def _():
            load(n + 1).start()

        @pl.when(n >= OUT_SLOTS)
        def _():
            @pl.when(p < stages - 1)
            def _():
                hop(n - OUT_SLOTS).wait_send()

        one_layer(x_in.at[in_slot], y_out.at[out_slot], weights, scratch, head_dim)

        @pl.when((p > 0) & (n + IN_SLOTS < total))
        def _():
            pl.semaphore_signal(credit, inc=1, device_id=before, device_id_type=MESH)

        @pl.when(p < stages - 1)
        def _():
            @pl.when(n >= IN_SLOTS)
            def _():
                pl.semaphore_wait(credit, 1)

            hop(n).start()

        put = store(n)
        put.start()
        put.wait()

        @pl.when(n < n_single)
        def _():
            side(n).start()

        return carry

    lax.fori_loop(0, total, step, 0)

    @pl.when(p < stages - 1)
    def _():
        for n in range(total - OUT_SLOTS, total):
            hop(n).wait_send()

    for far, near in copies:
        far.wait_send()

    def finish(n, carry):
        side(n).wait_send()
        side(n).wait_recv()
        return carry

    lax.fori_loop(0, n_single, finish, 0)


def solution(mesh):
    stages = mesh.shape["pp"]
    weight_specs = (
        P("pp", None), P("pp", None),
        P("pp", None, None, "tp", None), P("pp", None, "tp", None),
        P("pp", "tp", None, None), P("pp", None),
        P("pp", None), P("pp", None),
        P("pp", None, "tp"), P("pp", "tp"),
        P("pp", "tp", None), P("pp", None),
    )

    def local_run(x_micro, g1, c1, w_qkv, b_qkv, w_out, b_out, g2, c2, w_up, b_up, w_down, b_down):
        micro, rows, seq, width = x_micro.shape
        count = micro * rows
        heads, head_dim = w_qkv.shape[3:]
        half_width = heads * head_dim
        half_ff = w_up.shape[2]
        n_dup = N_DUP
        n_single = (count - n_dup) // 2
        cfg = (stages, n_single, n_dup, head_dim)
        operands = (
            x_micro.reshape(count, seq, width),
            g1, c1, b_out, g2, c2, b_down,
            w_qkv.reshape(3, width, half_width),
            b_qkv.reshape(1, 3 * half_width),
            w_out.reshape(half_width, width),
            w_up.reshape(width, half_ff),
            b_up.reshape(1, half_ff),
            w_down.reshape(half_ff, width),
        )
        anywhere = pl.BlockSpec(memory_space=pl.ANY)
        vmem = pl.BlockSpec(memory_space=pltpu.VMEM)
        out = pl.pallas_call(
            functools.partial(kernel, cfg),
            out_shape=jax.ShapeDtypeStruct((count, seq, width), BF16),
            in_specs=[anywhere] + [vmem] * 6 + [anywhere] * 6,
            out_specs=anywhere,
            scratch_shapes=[
                pltpu.VMEM((width, 3 * width), BF16),
                pltpu.VMEM((2, 1, 3 * half_width), BF16),
                pltpu.VMEM((1, 3 * width), F32),
                pltpu.VMEM((width, width), BF16),
                pltpu.VMEM((2, width, half_ff), BF16),
                pltpu.VMEM((2, 1, half_ff), BF16),
                pltpu.VMEM((2 * half_ff, width), BF16),
                pltpu.VMEM((IN_SLOTS, seq, width), BF16),
                pltpu.VMEM((OUT_SLOTS, seq, width), BF16),
                pltpu.VMEM((seq, width), BF16),
                pltpu.VMEM((seq, 3 * width), BF16),
                pltpu.VMEM((seq, width), BF16),
                pltpu.VMEM((seq, width), BF16),
                pltpu.VMEM((seq, 2 * half_ff), BF16),
                pltpu.SemaphoreType.DMA((8,)),
                pltpu.SemaphoreType.DMA((8,)),
                pltpu.SemaphoreType.DMA((8,)),
                pltpu.SemaphoreType.DMA((IN_SLOTS,)),
                pltpu.SemaphoreType.DMA((OUT_SLOTS,)),
                pltpu.SemaphoreType.DMA((OUT_SLOTS,)),
                pltpu.SemaphoreType.DMA((n_single,)),
                pltpu.SemaphoreType.DMA((n_single,)),
                pltpu.SemaphoreType.REGULAR,
            ],
            compiler_params=pltpu.CompilerParams(
                collective_id=0, has_side_effects=True, vmem_limit_bytes=60 * 2**20
            ),
        )(*operands)
        return out.reshape(1, micro, rows, seq, width)

    return jax.shard_map(
        local_run,
        mesh=mesh,
        in_specs=(P(None, "dp", None, None),) + weight_specs,
        out_specs=P("pp", None, "dp", None, None),
        check_vma=False,
    )
```

time: 7830 us -> 1080 us (0.14); the launches traced: 7740 us -> 1080 us
  waiting for transfers between devices: 5700 us -> 0 us
  matrix products: 1390 us -> 0 us
  Pallas kernels: 0 us -> 1030 us
  other arithmetic: 458 us -> 0 us
  local copies, waits for them, and re-layouts: 156 us -> 54.9 us
    psum x22 -> x0, waiting for transfers between devices: 5530 us -> none  [the longest x11 3250 us: stage_layer(): lax.psum(attn_part, 'tp').astype(jnp.float32) + b_out.astype(jnp.float32)]
    pallas_call x0 -> x1, Pallas kernels: none -> 1030 us  [local_run(): pl.pallas_call(functools.partial(kernel, cfg), out_shape=jax.ShapeDtypeSt...]
    dot_general x44 -> x0, matrix products: 1020 us -> none  [the longest x11 337 us: stage_layer(): jnp.einsum('crif,ife->cre', context, w_out, preferred_element_type=jnp.fl...]
    sub x11 -> x0, matrix products: 373 us -> none  [stage_layer(): jax.nn.softmax(jnp.where(causal, scores, -1e+30), axis=-1)]
    reduce_sum x44 -> x0, other arithmetic: 251 us -> none  [the longest x22 178 us: layer_norm(): row_mean = jnp.mean(act_f32, axis=-1, keepdims=True)]
    dynamic_update_slice x11 -> x0, other arithmetic: 198 us -> none  [time_step(): lax.dynamic_update_index_in_dim(out_buf, jnp.where(is_valid, stage_out, o...]
    ppermute x11 -> x0, waiting for transfers between devices: 172 us -> none  [time_step(): received = lax.ppermute(stage_out, 'pp', shift_pairs)]
    dynamic_slice x11 -> x0, local copies, waits for them, and re-layouts: 87.5 us -> none  [time_step(): old_slot = lax.dynamic_index_in_dim(out_buf, slot_idx, 0, keepdims=False)]
  transfers between devices with their start and end apart: 33 -> 0, of which waited for: 33 -> 0; matrix products, arithmetic and copies ran while one was open for 1% -> 0% of each run, Pallas kernels for 0% -> 0%
where the time goes in v1:
time: 1080 us
  Pallas kernels  1030 us (95%)
  local copies, waits for them, and re-layouts  54.9 us (5%)
    pallas_call x1, Pallas kernels, local_run(): pl.pallas_call(functools.partial(kernel, cfg), out_shape=jax.ShapeDtypeSt...  1030 us
    unnamed x1, local copies, waits for them, and re-layouts  49.7 us

profile of v1, /device:TPU:3, one launch (start us, length us, event | category | flops | bytes accessed | tf_op | source)
XLA Modules:
  0.0 1082.4 jit_solution(8051409948662329188)
XLA Ops:
  0.0 1.4 reshape.23.bqkv_half
  1.4 3.8 copy.15.qkv_half
  5.2 1027.6 %shard_map.127 = bf16[96,512,768]{2,1,0:T(8,128)(2,1)} custom-call(bf16[96,512,768]{2,1,0:T(8,128)(2,1)} %bitcast.x_hbm, bf16[1,768]{1,0:T(2,128)(2,1)} %g1.1, bf16[1,768]{1,0:T(2,128)(2,1)} %c1.1, bf16[1,768]{1,0:T(2,128)(2,1)} %bout.1, bf16[1,768]{1,0:T(2,128)(2,1)} %g2.1, bf16[1,768]{1,0:T(2,128)(2,1)} %c2.1, bf16[1,768]{1,0:T(2,128)(2,1)} %bdown.1, ...), custom_call_target="tpu_custom_call" | custom-call | tf_op jit(solution)/shard_map/pallas_call | solution.py:262
  1032.8 49.7 %copy.17 = bf16[1,8,12,512,768]{4,3,2,1,0:T(8,128)(2,1)} copy(bf16[1,8,12,512,768]{4,3,2,1,0:T(8,128)(2,1)} %bitcast.5) | data formatting | bytes 150994944

commit v2 on v1

--- a/solution.py
+++ b/solution.py
@@ -12,11 +12,12 @@
 BF16 = jnp.bfloat16
 MESH = pl.DeviceIdType.MESH
 LN_EPS = 1e-5
-N_DUP = 0
+N_DUP = 16
 IN_SLOTS = 3
 OUT_SLOTS = 2
 QUERY_BLOCK = 256
 COL_BLOCK = 256
+ROW_BLOCK = 128
 GELU_C0 = math.sqrt(2.0 / math.pi)
 GELU_C1 = GELU_C0 * 0.044715
 
@@ -34,8 +35,7 @@
 
 
 def gelu(z):
-    half = 0.5 * z
-    return half + half * jnp.tanh(z * (GELU_C0 + GELU_C1 * (z * z)))
+    return z * jax.nn.sigmoid(z * (2.0 * GELU_C0 + 2.0 * GELU_C1 * (z * z)))
 
 
 def attention(qkv, ctx, head_dim):
@@ -45,57 +45,66 @@
     first = lax.broadcasted_iota(jnp.int32, (1, pair), 1) < head_dim
     zero = jnp.zeros((), BF16)
     block = QUERY_BLOCK
-    rows = lax.broadcasted_iota(jnp.int32, (block, block), 0)
-    cols = lax.broadcasted_iota(jnp.int32, (block, block), 1)
-    keep = jnp.concatenate([rows >= cols, rows >= cols], axis=0)
-    for p in range(width // pair):
-        lanes = slice(p * pair, (p + 1) * pair)
-        keys = qkv[:, width + p * pair : width + (p + 1) * pair]
-        values = qkv[:, 2 * width + p * pair : 2 * width + (p + 1) * pair]
-        for q0 in range(0, seq, block):
+    keep = lax.broadcasted_iota(jnp.int32, (block, block), 0) >= lax.broadcasted_iota(jnp.int32, (block, block), 1)
+    keep = jnp.concatenate([keep, keep], axis=0)
+    for q0 in range(seq - block, -1, -block):
+        for p in range(width // pair):
+            lanes = slice(p * pair, (p + 1) * pair)
+            keys = qkv[: q0 + block, width + p * pair : width + (p + 1) * pair]
+            values = qkv[: q0 + block, 2 * width + p * pair : 2 * width + (p + 1) * pair]
             q = qkv[q0 : q0 + block, lanes]
             q = jnp.concatenate([jnp.where(first, q, zero), jnp.where(first, zero, q)], axis=0)
-            scores = dot(q, keys[: q0 + block], 1, 1)
+            scores = dot(q, keys, 1, 1)
             diag = jnp.where(keep, scores[:, q0:], -1e30)
             scores = jnp.concatenate([scores[:, :q0], diag], axis=1) if q0 else diag
             top = jnp.max(scores, axis=-1, keepdims=True)
             probs = jnp.exp2((scores - top) * scale)
             total = jnp.sum(probs, axis=-1, keepdims=True)
-            out = dot(probs.astype(BF16), values[: q0 + block]) * (1.0 / total)
+            out = dot(probs.astype(BF16), values) * (1.0 / total)
             ctx[q0 : q0 + block, lanes] = jnp.where(first, out[:block], out[block:]).astype(BF16)
 
 
-def project_residual(lhs, weight, bias, resid, out):
+def project_residual(lhs, weight, bias, resid, out, rows):
     for n in range(0, out.shape[1], COL_BLOCK):
         cols = slice(n, n + COL_BLOCK)
-        part = (dot(lhs[...], weight[:, cols]) + bias[:, cols].astype(F32)).astype(BF16)
-        out[:, cols] = (resid[:, cols].astype(F32) + part.astype(F32)).astype(BF16)
-
-
-def one_layer(x, y, w, s, head_dim):
-    width = x.shape[1]
-    s["h"][...] = layer_norm(x[...], w["g1"][...], w["c1"][...])
-    for n in range(0, 3 * width, COL_BLOCK):
-        cols = slice(n, n + COL_BLOCK)
-        s["qkv"][:, cols] = (dot(s["h"][...], w["qkv"][:, cols]) + w["bqkv"][:, cols]).astype(BF16)
+        part = (dot(lhs[rows], weight[:, cols]) + bias[:, cols].astype(F32)).astype(BF16)
+        out[rows, cols] = (resid[rows, cols].astype(F32) + part.astype(F32)).astype(BF16)
+
+
+def one_layer(x, y, w, s, head_dim, between):
+    seq, width = x.shape
+    blocks = [slice(m, m + ROW_BLOCK) for m in range(0, seq, ROW_BLOCK)]
+    for rows in blocks:
+        s["h"][rows] = layer_norm(x[rows], w["g1"][...], w["c1"][...])
+        for n in range(0, 3 * width, COL_BLOCK):
+            cols = slice(n, n + COL_BLOCK)
+            s["qkv"][rows, cols] = (dot(s["h"][rows], w["qkv"][:, cols]) + w["bqkv"][:, cols]).astype(BF16)
+    between()
     attention(s["qkv"], s["ctx"], head_dim)
-    project_residual(s["ctx"], w["out"], w["bout"], x, s["x1"])
-    s["h"][...] = layer_norm(s["x1"][...], w["g2"][...], w["c2"][...])
+    for rows in blocks:
+        project_residual(s["ctx"], w["out"], w["bout"], x, s["x1"], rows)
+        s["h"][rows] = layer_norm(s["x1"][rows], w["g2"][...], w["c2"][...])
     half = w["up"].shape[2]
     for t in range(2):
         for n in range(0, half, COL_BLOCK):
-            z = dot(s["h"][...], w["up"][t, :, n : n + COL_BLOCK]) + w["bup"][t, :, n : n + COL_BLOCK].astype(F32)
-            s["u"][:, t * half + n : t * half + n + COL_BLOCK] = gelu(z).astype(BF16)
-    project_residual(s["u"], w["down"], w["bdown"], s["x1"], y)
+            for rows in blocks:
+                z = dot(s["h"][rows], w["up"][t, :, n : n + COL_BLOCK])
+                z = z + w["bup"][t, :, n : n + COL_BLOCK].astype(F32)
+                s["u"][rows, t * half + n : t * half + n + COL_BLOCK] = gelu(z).astype(BF16)
+    for n in range(0, width, COL_BLOCK):
+        for rows in blocks:
+            cols = slice(n, n + COL_BLOCK)
+            part = (dot(s["u"][rows], w["down"][:, cols]) + w["bdown"][:, cols].astype(F32)).astype(BF16)
+            y[rows, cols] = (s["x1"][rows, cols].astype(F32) + part.astype(F32)).astype(BF16)
 
 
 def kernel(
     cfg,
     x_hbm, g1, c1, bout, g2, c2, bdown, qkv_half, bqkv_half, out_half, up_half, bup_half, down_half,
     out_hbm,
-    w_qkv, b_qkv_raw, b_qkv, w_out, w_up, b_up, w_down,
+    w_qkv_raw, w_qkv, b_qkv_raw, b_qkv, w_out, w_up, b_up, w_down,
     x_in, y_out, h, qkv, ctx, x1, u,
-    w_local, w_send, w_recv, in_sem, store_sem, hop_sem, side_send, side_recv, credit,
+    w_local, w_send, w_recv, in_sem, store_sem, hop_sem, side_send, side_recv, credit, turn,
 ):
     stages, n_single, n_dup, head_dim = cfg
     total = n_single + n_dup
@@ -112,22 +121,28 @@
         pl.semaphore_signal(barrier, inc=1, device_id=peer, device_id_type=MESH)
     pl.semaphore_wait(barrier, 3)
 
-    pieces = []
-    for c in range(3):
-        at = pl.multiple_of(c * width + t * half_width, 128)
-        pieces.append((qkv_half.at[c], w_qkv.at[:, pl.ds(at, half_width)]))
+    half_ff = down_half.shape[0]
+    mine = pl.ds(pl.multiple_of(t * half_width, 128), half_width)
+    pieces = [(qkv_half.at[c], w_qkv_raw.at[c, mine]) for c in range(3)]
     pieces.append((bqkv_half, b_qkv_raw.at[t]))
-    pieces.append((out_half, w_out.at[pl.ds(pl.multiple_of(t * half_width, 128), half_width)]))
+    pieces.append((out_half, w_out.at[mine]))
+    pieces.append((bup_half, b_up.at[t]))
     pieces.append((up_half, w_up.at[t]))
-    pieces.append((bup_half, b_up.at[t]))
-    pieces.append((down_half, w_down.at[pl.ds(pl.multiple_of(t * down_half.shape[0], 128), down_half.shape[0])]))
-    copies = []
+    pieces.append((down_half, w_down.at[pl.ds(pl.multiple_of(t * half_ff, 128), half_ff)]))
+    near, far = [], []
     for i, (src, dst) in enumerate(pieces):
-        far = pltpu.make_async_remote_copy(src, dst, w_send.at[i], w_recv.at[i], device_id=other, device_id_type=MESH)
-        near = pltpu.make_async_copy(src, dst, w_local.at[i])
-        far.start()
-        near.start()
-        copies.append((far, near))
+        near.append(pltpu.make_async_copy(src, dst, w_local.at[i]))
+        far.append(
+            pltpu.make_async_remote_copy(src, dst, w_send.at[i], w_recv.at[i], device_id=other, device_id_type=MESH)
+        )
+        near[-1].start()
+
+    @pl.when(lax.rem(p, 2) == 1)
+    def _():
+        pl.semaphore_wait(turn, 1)
+
+    for copy in far:
+        copy.start()
 
     def row_of(n):
         dup = n // n_single
@@ -157,13 +172,28 @@
     def _():
         load(0).start()
 
-    for far, near in copies:
-        near.wait()
-        far.wait_recv()
+    def arrived(i):
+        near[i].wait()
+        far[i].wait_recv()
+
+    for i in range(4):
+        arrived(i)
     for c in range(3):
+        for m in range(0, width, COL_BLOCK):
+            w_qkv[:, c * width + m : c * width + m + COL_BLOCK] = w_qkv_raw[c, m : m + COL_BLOCK, :].T
         for k in range(2):
-            at = c * width + k * half_width
-            b_qkv[:, at : at + half_width] = b_qkv_raw[k, :, c * half_width : (c + 1) * half_width].astype(F32)
+            for head in range(half_width // head_dim):
+                at = c * width + k * half_width + head * head_dim
+                b_qkv[:, at : at + head_dim] = b_qkv_raw[k, c, head : head + 1, :].astype(F32)
+    for copy in far:
+        copy.wait_send()
+
+    @pl.when(lax.rem(p, 2) == 0)
+    def _():
+        pl.semaphore_signal(turn, inc=1, device_id=after, device_id_type=MESH)
+
+    for i in range(4, len(far)):
+        arrived(i)
 
     weights = dict(
         g1=g1, c1=c1, qkv=w_qkv, bqkv=b_qkv, out=w_out, bout=bout, g2=g2, c2=c2,
@@ -171,6 +201,13 @@
     )
     scratch = dict(h=h, qkv=qkv, ctx=ctx, x1=x1, u=u)
 
+    def publish(n):
+        store(n).wait()
+
+        @pl.when(n < n_single)
+        def _():
+            side(n).start()
+
     def step(n, carry):
         in_slot, out_slot = lax.rem(n, IN_SLOTS), lax.rem(n, OUT_SLOTS)
         load(n).wait()
@@ -179,45 +216,40 @@
         def _():
             load(n + 1).start()
 
-        @pl.when(n >= OUT_SLOTS)
-        def _():
-            @pl.when(p < stages - 1)
+        @pl.when((n >= OUT_SLOTS) & (p < stages - 1))
+        def _():
+            hop(n - OUT_SLOTS).wait_send()
+
+        def between():
+            @pl.when(n >= 1)
             def _():
-                hop(n - OUT_SLOTS).wait_send()
-
-        one_layer(x_in.at[in_slot], y_out.at[out_slot], weights, scratch, head_dim)
+                publish(n - 1)
+
+        one_layer(x_in.at[in_slot], y_out.at[out_slot], weights, scratch, head_dim, between)
+
+        store(n).start()
+
+        @pl.when((p < stages - 1) & (n >= IN_SLOTS))
+        def _():
+            pl.semaphore_wait(credit, 1)
+
+        @pl.when(p < stages - 1)
+        def _():
+            hop(n).start()
 
         @pl.when((p > 0) & (n + IN_SLOTS < total))
         def _():
             pl.semaphore_signal(credit, inc=1, device_id=before, device_id_type=MESH)
 
-        @pl.when(p < stages - 1)
-        def _():
-            @pl.when(n >= IN_SLOTS)
-            def _():
-                pl.semaphore_wait(credit, 1)
-
-            hop(n).start()
-
-        put = store(n)
-        put.start()
-        put.wait()
-
-        @pl.when(n < n_single)
-        def _():
-            side(n).start()
-
         return carry
 
     lax.fori_loop(0, total, step, 0)
+    publish(total - 1)
 
     @pl.when(p < stages - 1)
     def _():
         for n in range(total - OUT_SLOTS, total):
             hop(n).wait_send()
-
-    for far, near in copies:
-        far.wait_send()
 
     def finish(n, carry):
         side(n).wait_send()
@@ -250,8 +282,8 @@
         operands = (
             x_micro.reshape(count, seq, width),
             g1, c1, b_out, g2, c2, b_down,
-            w_qkv.reshape(3, width, half_width),
-            b_qkv.reshape(1, 3 * half_width),
+            w_qkv.reshape(3, width, heads, head_dim).transpose(0, 2, 3, 1).reshape(3, half_width, width),
+            b_qkv.reshape(3, heads, head_dim),
             w_out.reshape(half_width, width),
             w_up.reshape(width, half_ff),
             b_up.reshape(1, half_ff),
@@ -265,8 +297,9 @@
             in_specs=[anywhere] + [vmem] * 6 + [anywhere] * 6,
             out_specs=anywhere,
             scratch_shapes=[
+                pltpu.VMEM((3, width, width), BF16),
                 pltpu.VMEM((width, 3 * width), BF16),
-                pltpu.VMEM((2, 1, 3 * half_width), BF16),
+                pltpu.VMEM((2, 3, heads, head_dim), BF16),
                 pltpu.VMEM((1, 3 * width), F32),
                 pltpu.VMEM((width, width), BF16),
                 pltpu.VMEM((2, width, half_ff), BF16),
@@ -288,6 +321,7 @@
                 pltpu.SemaphoreType.DMA((n_single,)),
                 pltpu.SemaphoreType.DMA((n_single,)),
                 pltpu.SemaphoreType.REGULAR,
+                pltpu.SemaphoreType.REGULAR,
             ],
             compiler_params=pltpu.CompilerParams(
                 collective_id=0, has_side_effects=True, vmem_limit_bytes=60 * 2**20

time: 1080 us -> 948 us (0.88)
  Pallas kernels: 1030 us -> 898 us
    pallas_call x1, Pallas kernels: 1030 us -> 898 us  [local_run(): pl.pallas_call(functools.partial(kernel, cfg), out_shape=jax.ShapeDtypeSt...]
where the time goes in v2:
time: 948 us
  Pallas kernels  898 us (95%)
  local copies, waits for them, and re-layouts  49.7 us (5%)
    pallas_call x1, Pallas kernels, local_run(): pl.pallas_call(functools.partial(kernel, cfg), out_shape=jax.ShapeDtypeSt...  898 us
    unnamed x1, local copies, waits for them, and re-layouts  49.7 us

profile of v2, /device:TPU:3, one launch (start us, length us, event | category | flops | bytes accessed | tf_op | source)
XLA Modules:
  0.0 948.2 jit_solution(10870160078690311648)
XLA Ops:
  0.0 898.5 %shard_map.127 = bf16[96,512,768]{2,1,0:T(8,128)(2,1)} custom-call(bf16[96,512,768]{2,1,0:T(8,128)(2,1)} %bitcast.x_hbm, bf16[1,768]{1,0:T(2,128)(2,1)} %g1.1, bf16[1,768]{1,0:T(2,128)(2,1)} %c1.1, bf16[1,768]{1,0:T(2,128)(2,1)} %bout.1, bf16[1,768]{1,0:T(2,128)(2,1)} %g2.1, bf16[1,768]{1,0:T(2,128)(2,1)} %c2.1, bf16[1,768]{1,0:T(2,128)(2,1)} %bdown.1, ...), custom_call_target="tpu_custom_call" | custom-call | tf_op jit(solution)/shard_map/pallas_call | solution.py:294
  898.5 49.7 %copy.15 = bf16[1,8,12,512,768]{4,3,2,1,0:T(8,128)(2,1)} copy(bf16[1,8,12,512,768]{4,3,2,1,0:T(8,128)(2,1)} %bitcast.8) | data formatting | bytes 150994944

commit v3 on v2

--- a/solution.py
+++ b/solution.py
@@ -12,7 +12,7 @@
 BF16 = jnp.bfloat16
 MESH = pl.DeviceIdType.MESH
 LN_EPS = 1e-5
-N_DUP = 16
+N_DUP = 18
 IN_SLOTS = 3
 OUT_SLOTS = 2
 QUERY_BLOCK = 256
@@ -144,9 +144,18 @@
     for copy in far:
         copy.start()
 
+    def dups_before(n):
+        return n * n_dup // total
+
+    def single_index(n):
+        return n - dups_before(n)
+
+    def is_dup(n):
+        return dups_before(n + 1) - dups_before(n)
+
     def row_of(n):
-        dup = n // n_single
-        return n + (1 - dup) * t * n_single + dup * n_single
+        dup = is_dup(n)
+        return dup * (2 * n_single + dups_before(n)) + (1 - dup) * (t * n_single + single_index(n))
 
     def load(n):
         slot = lax.rem(n, IN_SLOTS)
@@ -162,10 +171,10 @@
             y_out.at[src], x_in.at[dst], hop_sem.at[src], in_sem.at[dst], device_id=after, device_id_type=MESH
         )
 
-    def side(n):
-        row = row_of(n)
+    def side(k):
+        row = t * n_single + k
         return pltpu.make_async_remote_copy(
-            out_hbm.at[row], out_hbm.at[row], side_send.at[n], side_recv.at[n], device_id=other, device_id_type=MESH
+            out_hbm.at[row], out_hbm.at[row], side_send.at[k], side_recv.at[k], device_id=other, device_id_type=MESH
         )
 
     @pl.when(p == 0)
@@ -185,7 +194,7 @@
             for head in range(half_width // head_dim):
                 at = c * width + k * half_width + head * head_dim
                 b_qkv[:, at : at + head_dim] = b_qkv_raw[k, c, head : head + 1, :].astype(F32)
-    for copy in far:
+    for copy in far[:6]:
         copy.wait_send()
 
     @pl.when(lax.rem(p, 2) == 0)
@@ -204,9 +213,9 @@
     def publish(n):
         store(n).wait()
 
-        @pl.when(n < n_single)
-        def _():
-            side(n).start()
+        @pl.when(is_dup(n) == 0)
+        def _():
+            side(single_index(n)).start()
 
     def step(n, carry):
         in_slot, out_slot = lax.rem(n, IN_SLOTS), lax.rem(n, OUT_SLOTS)
@@ -251,9 +260,12 @@
         for n in range(total - OUT_SLOTS, total):
             hop(n).wait_send()
 
-    def finish(n, carry):
-        side(n).wait_send()
-        side(n).wait_recv()
+    for copy in far[6:]:
+        copy.wait_send()
+
+    def finish(k, carry):
+        side(k).wait_send()
+        side(k).wait_recv()
         return carry
 
     lax.fori_loop(0, n_single, finish, 0)

time: 948 us -> 916 us (0.966)
  Pallas kernels: 898 us -> 866 us
    pallas_call x1, Pallas kernels: 898 us -> 866 us  [local_run(): pl.pallas_call(functools.partial(kernel, cfg), out_shape=jax.ShapeDtypeSt...]
where the time goes in v3:
time: 916 us
  Pallas kernels  866 us (95%)
  local copies, waits for them, and re-layouts  49.7 us (5%)
    pallas_call x1, Pallas kernels, local_run(): pl.pallas_call(functools.partial(kernel, cfg), out_shape=jax.ShapeDtypeSt...  866 us
    unnamed x1, local copies, waits for them, and re-layouts  49.7 us

profile of v3, /device:TPU:3, one launch (start us, length us, event | category | flops | bytes accessed | tf_op | source)
XLA Modules:
  0.0 915.6 jit_solution(3558181923237250678)
XLA Ops:
  0.0 866.0 %shard_map.127 = bf16[96,512,768]{2,1,0:T(8,128)(2,1)} custom-call(bf16[96,512,768]{2,1,0:T(8,128)(2,1)} %bitcast.x_hbm, bf16[1,768]{1,0:T(2,128)(2,1)} %g1.1, bf16[1,768]{1,0:T(2,128)(2,1)} %c1.1, bf16[1,768]{1,0:T(2,128)(2,1)} %bout.1, bf16[1,768]{1,0:T(2,128)(2,1)} %g2.1, bf16[1,768]{1,0:T(2,128)(2,1)} %c2.1, bf16[1,768]{1,0:T(2,128)(2,1)} %bdown.1, ...), custom_call_target="tpu_custom_call" | custom-call | tf_op jit(solution)/shard_map/pallas_call | solution.py:306
  866.0 49.7 %copy.15 = bf16[1,8,12,512,768]{4,3,2,1,0:T(8,128)(2,1)} copy(bf16[1,8,12,512,768]{4,3,2,1,0:T(8,128)(2,1)} %bitcast.8) | data formatting | bytes 150994944
